TPU v7x, 32 devices: a whole 2x2x4 slice. The times are simulated.
32 devices in a mesh: epoch: 4 (over y, x), blend: 8 (over z, core).
Axes of the slice: x: 2, y: 2, z: 4, core: 2. Of those that a mesh axis runs over, the one named last changes fastest.
Arguments:
- visit_flux: bfloat16 [16, 32, 6, 16384], P('epoch', None, None, 'blend'), may hold values from -6 to 6
- visit_precision: bfloat16 [16, 32, 6, 16384], P('epoch', None, None, 'blend'), may hold values from 0.25 to 4
- visit_live: int32 [16, 32], P('epoch'), may hold values 0 or 1
- footprint: int32 [32, 8, 16384], P('blend', None, 'epoch'), may hold values 0 or 1
- source_count: int32 [32], P('blend'), may hold values from 1 to 8
- spectra_init: float32 [32, 8, 6], P('blend'), may hold values from 0.2 to 1.2
- morphology_init: float32 [32, 8, 16384], P('blend', None, 'epoch'), may hold values from 0 to 0.25
Outputs:
- coadd_flux: float32 [32, 6, 16384], P('blend', None, 'epoch')
- spectra: float32 [32, 8, 6], P('blend')
- morphology: float32 [32, 8, 16384], P('blend', None, 'epoch')
All inputs are finite; a program needn't handle non-finite values. No bound on the sum of `visit_live` or of `footprint` on one device may be relied on, other than what follows from the above.
Results may differ from a plain program's by a relative error of at most 0.0003.
Values sent between devices are 32-bit elements; how exact they have to be, the bound alone decides.
A program may use at most 64 MiB of HBM per device.

v0:
```python
import functools

import jax
import jax.numpy as jnp
from jax import lax
from jax.experimental import pallas as pl
from jax.experimental.pallas import tpu as pltpu
from jax.sharding import PartitionSpec as P

ITERS = 2


LANES = 128
MESH = pl.DeviceIdType.MESH


def factors(count):
    rows = max(d for d in range(1, count + 1) if count % d == 0 and d * d <= count)
    return rows, count // rows


def coadd_kernel(
    flux_hbm, prec_hbm, live_ref, foot_hbm, count_ref, spec_ref, morph_hbm,
    coadd_ref, spec_out, morph_ref,
    flux_v, prec_v, foot_v, flux_c, cover,
    stage, land1, part, land2, final, pieces, spectra, step_ref, acc, sums,
    in_sem, side_sem, s1_send, s1_recv, s2_send, s2_recv, s3_send, s3_recv, ps_send, ps_recv,
    *, ne, nb, ny, nx,
):
    visits, bands, every_blend, block = flux_hbm.shape
    owned, slots, pix_part = morph_hbm.shape
    chunks = flux_v.shape[0]
    width = block // chunks
    per_dest = pix_part // block
    held = per_dest * owned
    e = lax.axis_index("epoch")
    j = lax.axis_index("blend")
    y, x = e // nx, e % nx
    home_e = j // per_dest
    home_slot = j % per_dest
    f32 = jnp.float32

    def in_copy(q):
        window = pl.ds(q * width, width)
        return (
            pltpu.make_async_copy(prec_hbm.at[:, :, :, window], prec_v.at[q], in_sem.at[0, q]),
            pltpu.make_async_copy(flux_hbm.at[:, :, :, window], flux_v.at[q], in_sem.at[1, q]),
        )

    side = []
    for s in range(per_dest):
        for b in range(owned):
            row = s * owned + b
            window = pl.ds(s * block, block)
            side.append(pltpu.make_async_copy(
                foot_hbm.at[b, :, window], foot_v.at[:, row, :], side_sem.at[0, row]))
            side.append(pltpu.make_async_copy(
                morph_hbm.at[b, :, window], morph_ref.at[:, row, :], side_sem.at[1, row]))

    for q in range(chunks):
        for copy in in_copy(q):
            copy.start()

    barrier = pltpu.get_barrier_semaphore()
    total = ne * nb
    mine = e * nb + j

    def greet(d, carry):
        other = lax.rem(mine + d, total)
        pl.semaphore_signal(
            barrier, inc=1, device_id=(other // nb, lax.rem(other, nb)), device_id_type=MESH
        )
        return carry

    lax.fori_loop(1, total, greet, 0)

    square_r = lax.broadcasted_iota(jnp.int32, (every_blend, every_blend), 0)
    square_c = lax.broadcasted_iota(jnp.int32, (every_blend, every_blend), 1)
    lives = []
    for v in range(visits):
        row = jnp.broadcast_to(live_ref[v : v + 1, :].astype(f32), (every_blend, every_blend))
        column = jnp.sum(jnp.where(square_r == square_c, row, 0.0), axis=1, keepdims=True)
        lives.append(jnp.broadcast_to(column, (every_blend, LANES)))

    def local_sum(q):
        for copy in in_copy(q):
            copy.wait()

        def one(c, carry):
            for p in range(ne):
                lanes = slice(p * LANES, (p + 1) * LANES)
                py, px = p // nx, p % nx
                num = None
                for v in range(visits):
                    w = prec_v[q, v, c, :, lanes].astype(f32) * lives[v]
                    n = w * flux_v[q, v, c, :, lanes].astype(f32)
                    num, wsum = (n, w) if num is None else (num + n, wsum + w)
                stage[0, q, px * ny + py, c] = num
                stage[1, q, py * nx + px, c] = wsum
            return carry

        lax.fori_loop(0, bands, one, 0)

    def line(a, first):
        along_x = (a == 0) == first
        return (x, nx) if along_x else (y, ny)

    def device_at(a, first, where):
        along_x = (a == 0) == first
        return (y * nx + where if along_x else where * nx + x, j)

    def s1(a, q, d):
        at, n = line(a, True)
        other = line(a, False)[1]
        to = lax.rem(at + d, n)
        return pltpu.make_async_remote_copy(
            src_ref=stage.at[a, q, pl.ds(to * other, other)],
            dst_ref=land1.at[a, q, d - 1],
            send_sem=s1_send.at[a, q, d - 1], recv_sem=s1_recv.at[a, q, d - 1],
            device_id=device_at(a, True, to), device_id_type=MESH,
        )

    def s2(a, q, d):
        at, n = line(a, False)
        to = lax.rem(at + d, n)
        return pltpu.make_async_remote_copy(
            src_ref=part.at[a, q, to],
            dst_ref=land2.at[a, q, d - 1],
            send_sem=s2_send.at[a, q, d - 1], recv_sem=s2_recv.at[a, q, d - 1],
            device_id=device_at(a, False, to), device_id_type=MESH,
        )

    def s1_start(q):
        for a in range(2):
            for d in range(1, line(a, True)[1]):
                s1(a, q, d).start()

    def s2_start(q):
        for a in range(2):
            at, n = line(a, True)
            others = line(a, False)[1]
            for d in range(1, n):
                s1(a, q, d).wait_recv()

            def add(c, carry):
                for o in range(others):
                    v = stage[a, q, at * others + o, c]
                    for d in range(1, n):
                        v = v + land1[a, q, d - 1, o, c]
                    part[a, q, o, c] = v
                return carry

            lax.fori_loop(0, bands, add, 0)
            for d in range(1, others):
                s2(a, q, d).start()

    here = home_e == e

    def landing(q):
        lanes = pl.ds(pl.multiple_of(e * LANES, LANES), LANES)
        return pieces.at[q, :, :, home_slot, :, lanes]

    def s3_local(q):
        return pltpu.make_async_copy(final.at[q, j], landing(q), s3_recv.at[q])

    def s3_remote(q, to):
        return pltpu.make_async_remote_copy(
            src_ref=final.at[q, to], dst_ref=landing(q),
            send_sem=s3_send.at[q, to], recv_sem=s3_recv.at[q],
            device_id=(home_e, to), device_id_type=MESH,
        )

    def s3_start(q):
        for a in range(2):
            at, n = line(a, False)
            for d in range(1, n):
                s2(a, q, d).wait_recv()

            def add(c, carry):
                v = part[a, q, at, c]
                for d in range(1, n):
                    v = v + land2[a, q, d - 1, c]
                for to in range(nb):
                    final[q, to, a, c] = v[to * owned : (to + 1) * owned, :]
                return carry

            lax.fori_loop(0, bands, add, 0)

        def send(d, carry):
            s3_remote(q, lax.rem(j + d, nb)).start()
            return carry

        lax.fori_loop(1, nb, send, 0)

        @pl.when(here)
        def _():
            s3_local(q).start()

        @pl.when(jnp.logical_not(here))
        def _():
            s3_remote(q, j).start()

    sub = lax.broadcasted_iota(jnp.int32, (held, LANES), 0)
    lane = lax.broadcasted_iota(jnp.int32, (held, LANES), 1)
    count = jnp.zeros((held, LANES), jnp.int32)
    for b in range(owned):
        count = jnp.where(lax.rem(sub, owned) == b, count_ref[b], count)
    live_count = count.astype(f32)

    def steps():
        for k in range(slots):
            norm = None
            for c in range(bands):
                s = spectra[k, c]
                norm = s * s if norm is None else norm + s * s
            step_ref[k] = 1.0 / (1.0 + live_count * norm)

    group = 2

    def deblend(start, first):
        runs = [
            pl.ds(pl.multiple_of(start + t * LANES, LANES), LANES) for t in range(group)
        ]

        def masks(k):
            live = jnp.where(count > k, 1.0, 0.0).astype(f32)
            return [foot_v[k, :, px].astype(f32) * live for px in runs]

        def residual(morph):
            res = []
            for c in range(bands):
                model = [None] * group
                for k in range(slots):
                    s = spectra[k, c]
                    for t in range(group):
                        v = s * morph[k][t]
                        model[t] = v if k == 0 else model[t] + v
                res.append([
                    cover[c, :, px] * (flux_c[c, :, px] - model[t]) for t, px in enumerate(runs)
                ])
            return res

        morph = []
        for k in range(slots):
            m = [morph_ref[k, :, px] for px in runs]
            morph.append([a * b for a, b in zip(m, masks(k))] if first else m)
        res = residual(morph)
        for k in range(slots):
            mask = masks(k)
            grad = [None] * group
            for c in range(bands):
                s = spectra[k, c]
                for t in range(group):
                    v = s * res[c][t]
                    grad[t] = v if c == 0 else grad[t] + v
            step = step_ref[k]
            for t, px in enumerate(runs):
                m = jnp.maximum(0.0, morph[k][t] + grad[t] * step) * mask[t]
                morph[k][t] = m
                morph_ref[k, :, px] = m
        res = residual(morph)
        for k in range(slots):
            for c in range(bands):
                v = acc[k, c]
                for t in range(group):
                    v = v + morph[k][t] * res[c][t]
                acc[k, c] = v
            v = acc[k, bands]
            for t in range(group):
                v = v + morph[k][t] * morph[k][t]
            acc[k, bands] = v

    def finish(q):
        pltpu.make_async_copy(pieces.at[q], pieces.at[q], s3_recv.at[q]).wait()
        at = slice(q * width, (q + 1) * width)

        def unpack(c, carry):
            for s in range(per_dest):
                rows = slice(s * owned, (s + 1) * owned)
                wsum = pieces[q, 1, c, s]
                inv = 1.0 / (1.0 + wsum)
                flux = pieces[q, 0, c, s] * inv
                coadd_ref[c, :, s * block + q * width : s * block + (q + 1) * width] = flux
                flux_c[c, rows, at] = flux
                cover[c, rows, at] = wsum * inv
            return carry

        lax.fori_loop(0, bands, unpack, 0)

        def go(i, carry):
            deblend(q * width + i * (group * LANES), True)
            return carry

        lax.fori_loop(0, width // (group * LANES), go, 0)

    def ps_copy(it, d):
        to = lax.rem(e + d, ne)
        return pltpu.make_async_remote_copy(
            src_ref=sums.at[it, 0], dst_ref=sums.at[it, d],
            send_sem=ps_send.at[it, d - 1], recv_sem=ps_recv.at[it, d - 1],
            device_id=(to, j), device_id_type=MESH,
        )

    def update(it):
        packed = jnp.zeros((held, LANES), f32)
        for k in range(slots):
            for c in range(bands + 1):
                whole = jnp.sum(acc[k, c], axis=1, keepdims=True)
                packed = jnp.where(lane == k * (bands + 1) + c, whole, packed)
        sums[it, 0] = packed
        for d in range(1, ne):
            ps_copy(it, d).start()
        for d in range(1, ne):
            ps_copy(it, d).wait_recv()
        whole = None
        for o in range(ne):
            v = sums[it, lax.rem(e - o + ne, ne)]
            whole = v if whole is None else whole + v
        one = whole[0:owned, :]
        for s in range(1, per_dest):
            one = one + whole[s * owned : (s + 1) * owned, :]
        whole = jnp.concatenate([one] * per_dest, axis=0)
        for k in range(slots):
            at = k * (bands + 1)
            norm = jnp.broadcast_to(whole[:, at + bands : at + bands + 1], (held, LANES))
            scale = 1.0 / (1.0 + live_count * norm)
            for c in range(bands):
                grad = jnp.broadcast_to(whole[:, at + c : at + c + 1], (held, LANES))
                spectra[k, c] = jnp.maximum(0.0, spectra[k, c] + grad * scale)

    local_sum(0)
    pl.semaphore_wait(barrier, total - 1)
    s1_start(0)
    if chunks > 1:
        local_sum(1)
        s1_start(1)
    for copy in side:
        copy.start()

    acc[...] = jnp.zeros_like(acc)
    for k in range(slots):
        for c in range(bands):
            start = jnp.broadcast_to(spec_ref[c, :, k : k + 1], (owned, LANES))
            spectra[k, c] = jnp.concatenate([start] * per_dest, axis=0)
    steps()

    for q in range(chunks + 2):
        if q < chunks:
            s2_start(q)
        if q + 2 < chunks:
            local_sum(q + 2)
            s1_start(q + 2)
        if 0 <= q - 1 < chunks:
            s3_start(q - 1)
        if q == 2:
            for copy in side:
                copy.wait()
        if 0 <= q - 2 < chunks:
            finish(q - 2)

    update(0)
    for it in range(1, ITERS):
        steps()
        acc[...] = jnp.zeros_like(acc)

        def again(i, carry):
            deblend(i * (group * LANES), False)
            return carry

        lax.fori_loop(0, block // (group * LANES), again, 0)
        update(it)
    for c in range(bands):
        out = spectra[0, c]
        for k in range(1, slots):
            out = jnp.where(lane == k, spectra[k, c], out)
        spec_out[c] = out[0:owned, :slots]

    for q in range(chunks):
        for a in range(2):
            for d in range(1, line(a, True)[1]):
                s1(a, q, d).wait_send()
            for d in range(1, line(a, False)[1]):
                s2(a, q, d).wait_send()

        def sent(d, carry, q=q):
            s3_remote(q, lax.rem(j + d, nb)).wait_send()
            return carry

        lax.fori_loop(1, nb, sent, 0)

        @pl.when(jnp.logical_not(here))
        def _(q=q):
            s3_remote(q, j).wait_send()

    for it in range(ITERS):
        for d in range(1, ne):
            ps_copy(it, d).wait_send()


def hand_over(coadd_in, spec_in, morph_in, coadd_out, spec_out, morph_out, sems, row_sems):
    owned, _, pix_part = morph_out.shape
    _, held, block = morph_in.shape
    copies = [
        pltpu.make_async_copy(morph_in.at[:, row, :],
                              morph_out.at[row % owned, :, pl.ds(row // owned * block, block)],
                              row_sems.at[row])
        for row in range(held)
    ]
    copies.append(pltpu.make_async_copy(coadd_in, coadd_out, sems.at[0]))
    copies.append(pltpu.make_async_copy(spec_in, spec_out, sems.at[1]))
    for copy in copies:
        copy.start()
    for copy in copies:
        copy.wait()


def fused(ne, nb, visit_flux, visit_precision, visit_live, footprint, source_count, spectra_init,
          morphology_init):
    visits, every_blend, bands, block = visit_flux.shape
    owned, slots, pix_part = morphology_init.shape
    ny, nx = factors(ne)
    width = ne * LANES
    chunks = block // width
    per_dest = pix_part // block
    held = per_dest * owned
    hop = max(nx, ny) - 1
    line = max(nx, ny)
    f32 = jnp.float32
    vmem, smem, hbm = (pl.BlockSpec(memory_space=s) for s in (pltpu.VMEM, pltpu.SMEM, pl.ANY))
    dma = pltpu.SemaphoreType.DMA
    parts = pl.pallas_call(
        functools.partial(coadd_kernel, ne=ne, nb=nb, ny=ny, nx=nx),
        out_shape=(
            pltpu.VMEM((bands, owned, pix_part), f32),
            pltpu.VMEM((bands, owned, slots), f32),
            pltpu.VMEM((slots, held, block), f32),
        ),
        in_specs=[hbm, hbm, vmem, hbm, smem, vmem, hbm],
        out_specs=(vmem, vmem, vmem),
        scratch_shapes=[
            pltpu.VMEM((chunks, visits, bands, every_blend, width), visit_flux.dtype),
            pltpu.VMEM((chunks, visits, bands, every_blend, width), visit_precision.dtype),
            pltpu.VMEM((slots, held, block), jnp.int32),
            pltpu.VMEM((bands, held, block), f32),
            pltpu.VMEM((bands, held, block), f32),
            pltpu.VMEM((2, chunks, ne, bands, every_blend, LANES), f32),
            pltpu.VMEM((2, chunks, hop, line, bands, every_blend, LANES), f32),
            pltpu.VMEM((2, chunks, line, bands, every_blend, LANES), f32),
            pltpu.VMEM((2, chunks, hop, bands, every_blend, LANES), f32),
            pltpu.VMEM((chunks, nb, 2, bands, owned, LANES), f32),
            pltpu.VMEM((chunks, 2, bands, per_dest, owned, width), f32),
            pltpu.VMEM((slots, bands, held, LANES), f32),
            pltpu.VMEM((slots, held, LANES), f32),
            pltpu.VMEM((slots, bands + 1, held, LANES), f32),
            pltpu.VMEM((ITERS, ne, held, LANES), f32),
            dma((2, chunks)),
            dma((2, held)),
            dma((2, chunks, hop)),
            dma((2, chunks, hop)),
            dma((2, chunks, hop)),
            dma((2, chunks, hop)),
            dma((chunks, nb)),
            dma((chunks,)),
            dma((ITERS, ne - 1)),
            dma((ITERS, ne - 1)),
        ],
        compiler_params=pltpu.CompilerParams(
            collective_id=0, has_side_effects=True, vmem_limit_bytes=58 * 2**20
        ),
    )(visit_flux.transpose(0, 2, 1, 3), visit_precision.transpose(0, 2, 1, 3), visit_live,
      footprint, source_count, spectra_init.transpose(2, 0, 1), morphology_init)
    coadd, spectra, morphology = pl.pallas_call(
        hand_over,
        out_shape=(
            jax.ShapeDtypeStruct((bands, owned, pix_part), f32),
            jax.ShapeDtypeStruct((bands, owned, slots), f32),
            jax.ShapeDtypeStruct((owned, slots, pix_part), f32),
        ),
        in_specs=[vmem] * 3,
        out_specs=(hbm,) * 3,
        scratch_shapes=[dma((2,)), dma((held,))],
        compiler_params=pltpu.CompilerParams(vmem_limit_bytes=8 * 2**20),
    )(*parts)
    return coadd.transpose(1, 0, 2), spectra.transpose(1, 2, 0), morphology


def on_device(
    visit_flux, visit_precision, visit_live, footprint, source_count, spectra_init, morphology_init
):
    weights = visit_precision.astype(jnp.float32) * visit_live.astype(jnp.float32)[:, :, None, None]
    numerator = jnp.sum(weights * visit_flux.astype(jnp.float32), axis=0)
    weight_sum = jnp.sum(weights, axis=0)
    pix_part = morphology_init.shape[2]
    owned = morphology_init.shape[0]
    numerator, weight_sum = (
        lax.psum_scatter(numerator, "epoch", scatter_dimension=2, tiled=True),
        lax.psum_scatter(weight_sum, "epoch", scatter_dimension=2, tiled=True),
    )
    every_blend, band_count, piece = numerator.shape
    numerator = numerator.reshape(every_blend, band_count, 1, piece)
    weight_sum = weight_sum.reshape(every_blend, band_count, 1, piece)
    numerator, weight_sum = (
        lax.all_to_all(numerator, "blend", split_axis=0, concat_axis=2, tiled=True),
        lax.all_to_all(weight_sum, "blend", split_axis=0, concat_axis=2, tiled=True),
    )
    blocks = numerator.shape[2]
    numerator = numerator.reshape(owned, band_count, blocks, 1, piece)
    weight_sum = weight_sum.reshape(owned, band_count, blocks, 1, piece)
    numerator, weight_sum = (
        lax.all_to_all(numerator, "epoch", split_axis=2, concat_axis=3, tiled=True),
        lax.all_to_all(weight_sum, "epoch", split_axis=2, concat_axis=3, tiled=True),
    )
    numerator = numerator.reshape(owned, band_count, pix_part)
    weight_sum = weight_sum.reshape(owned, band_count, pix_part)
    coadd_flux = numerator / (1.0 + weight_sum)
    coverage = weight_sum / (1.0 + weight_sum)
    slots = footprint.shape[1]
    source_live = (jnp.arange(slots, dtype=jnp.int32)[None, :] < source_count[:, None]).astype(
        jnp.float32
    )
    footprint_mask = footprint.astype(jnp.float32) * source_live[:, :, None]
    live_count = source_count.astype(jnp.float32)
    morphology = morphology_init * footprint_mask
    spectra = spectra_init
    highest = lax.Precision.HIGHEST
    for iteration in range(ITERS):
        blend_model = jnp.einsum("bkc,bkp->bcp", spectra, morphology, precision=highest)
        residual = coverage * (coadd_flux - blend_model)
        morph_grad = jnp.einsum("bkc,bcp->bkp", spectra, residual, precision=highest)
        morph_step = 1.0 / (1.0 + live_count[:, None] * jnp.sum(spectra * spectra, axis=2))
        morphology = (
            jnp.maximum(0.0, morphology + morph_grad * morph_step[:, :, None]) * footprint_mask
        )
        blend_model = jnp.einsum("bkc,bkp->bcp", spectra, morphology, precision=highest)
        residual = coverage * (coadd_flux - blend_model)
        spectra_grad = jnp.einsum("bkp,bcp->bkc", morphology, residual, precision=highest)
        morph_norm = jnp.sum(morphology * morphology, axis=2)
        spectra_grad, morph_norm = lax.psum((spectra_grad, morph_norm), "epoch")
        spectra = jnp.maximum(
            0.0, spectra + spectra_grad / (1.0 + live_count[:, None] * morph_norm)[:, :, None]
        )
    return (coadd_flux, spectra, morphology)


def solution(mesh):
    ne, nb = mesh.shape["epoch"], mesh.shape["blend"]

    def step(visit_flux, visit_precision, visit_live, footprint, source_count, spectra_init,
             morphology_init):
        block, bands = visit_flux.shape[3], visit_flux.shape[2]
        owned, pix_part = morphology_init.shape[0], morphology_init.shape[2]
        ny, nx = factors(ne)
        fits = (
            block % (ne * LANES) == 0
            and pix_part % block == 0
            and min(ny, nx) > 1
            and morphology_init.shape[1] * (bands + 1) <= LANES
        )
        run = functools.partial(fused, ne, nb) if fits else on_device
        return run(visit_flux, visit_precision, visit_live, footprint, source_count, spectra_init,
                   morphology_init)

    in_specs = (
        P("epoch", None, None, "blend"),
        P("epoch", None, None, "blend"),
        P("epoch", None),
        P("blend", None, "epoch"),
        P("blend"),
        P("blend", None, None),
        P("blend", None, "epoch"),
    )
    out_specs = (P("blend", None, "epoch"), P("blend", None, None), P("blend", None, "epoch"))
    return jax.shard_map(
        step, mesh=mesh, in_specs=in_specs, out_specs=out_specs, check_vma=False
    )
```

profile of v0, /device:TPU:0, one launch (start us, length us, event | category | flops | bytes accessed | tf_op | source)
XLA Modules:
  0.0 57.4 jit_solution(11928125684936701673)
XLA Ops:
  0.6 55.7 %shard_map.94 = (f32[6,4,4096]{2,1,0:T(4,128)S(1)}, f32[6,4,8]{2,1,0:T(4,128)S(1)}, f32[8,8,2048]{2,1,0:T(8,128)S(1)}) custom-call(bf16[4,6,32,2048]{3,2,1,0:T(8,128)(2,1)} %bitcast.5, bf16[4,6,32,2048]{3,2,1,0:T(8,128)(2,1)} %bitcast.6, s32[4,32]{1,0:T(4,128)} %live_ref.1, s32[4,8,4096]{2,1,0:T(8,128)} %foot_hbm.1, s32[4]{0:T(128)} %count_ref.1, ...), custom_call_target="tpu_custom_call" | custom-call | tf_op jit(solution)/shard_map/pallas_call | solution.py:431
  56.4 1.0 %shard_map.95 = (f32[6,4,4096]{2,1,0:T(4,128)}, f32[6,4,8]{2,1,0:T(4,128)}, f32[4,8,4096]{2,1,0:T(8,128)}) custom-call(f32[6,4,4096]{2,1,0:T(4,128)S(1)} %get-tuple-element.9.coadd_in, f32[6,4,8]{2,1,0:T(4,128)S(1)} %get-tuple-element.10.spec_in, f32[8,8,2048]{2,1,0:T(8,128)S(1)} %get-tuple-element.11.morph_in), custom_call_target="tpu_custom_call" | custom-call | tf_op jit(solution)/shard_map/pallas_call | solution.py:472
where the time goes:
time: 57.6 us; the launch traced here: 57.4 us
  Pallas kernels  56.7 us (98%)
  between operations  0.64 us (1%)
    pallas_call x1, Pallas kernels, fused(): pl.pallas_call(functools.partial(coadd_kernel, ne=ne, nb=nb, ny=ny, nx=nx...  55.7 us

commit v1 on v0

--- a/solution.py
+++ b/solution.py
@@ -12,6 +12,8 @@
 
 LANES = 128
 MESH = pl.DeviceIdType.MESH
+AHEAD = 3
+LAG = 2
 
 
 def factors(count):
@@ -19,61 +21,95 @@
     return rows, count // rows
 
 
+def cut(chunks, bands):
+    half = max(1, bands // 2)
+    return [
+        (q, lo, min(bands, lo + half)) for q in range(chunks) for lo in range(0, bands, half)
+    ]
+
+
+def bits(count):
+    return [1 << k for k in range(count.bit_length() - 1)]
+
+
+def flip(at, bit):
+    return at + bit - 2 * bit * (at // bit % 2)
+
+
 def coadd_kernel(
-    flux_hbm, prec_hbm, live_ref, foot_hbm, count_ref, spec_ref, morph_hbm,
+    flux_hbm, prec_hbm, live_hbm, foot_hbm, count_hbm, spec_hbm, morph_hbm,
     coadd_ref, spec_out, morph_ref,
-    flux_v, prec_v, foot_v, flux_c, cover,
+    in_v, live_ref, foot_v, count_ref, spec_ref, flux_c, cover,
     stage, land1, part, land2, final, pieces, spectra, step_ref, acc, sums,
-    in_sem, side_sem, s1_send, s1_recv, s2_send, s2_recv, s3_send, s3_recv, ps_send, ps_recv,
-    *, ne, nb, ny, nx,
+    in_sem, side_sem, near_sem, send_sem, s1_recv, s2_recv, s3_recv, ps_recv,
+    *, ne, nb,
 ):
     visits, bands, every_blend, block = flux_hbm.shape
     owned, slots, pix_part = morph_hbm.shape
-    chunks = flux_v.shape[0]
+    chunks = in_v.shape[1]
     width = block // chunks
     per_dest = pix_part // block
     held = per_dest * owned
     e = lax.axis_index("epoch")
     j = lax.axis_index("blend")
-    y, x = e // nx, e % nx
+    y, x = e // 2, e % 2
     home_e = j // per_dest
     home_slot = j % per_dest
     f32 = jnp.float32
-
-    def in_copy(q):
-        window = pl.ds(q * width, width)
-        return (
-            pltpu.make_async_copy(prec_hbm.at[:, :, :, window], prec_v.at[q], in_sem.at[0, q]),
-            pltpu.make_async_copy(flux_hbm.at[:, :, :, window], flux_v.at[q], in_sem.at[1, q]),
-        )
-
+    work = cut(chunks, bands)
+    count_of = len(work)
+    loads = [w for w in work if w[0] == 0] + [(q, 0, bands) for q in range(1, chunks)]
+
+    small = [
+        pltpu.make_async_copy(src, dst, side_sem.at[k])
+        for k, (src, dst) in enumerate(
+            ((live_hbm, live_ref), (count_hbm, count_ref), (spec_hbm, spec_ref)))
+    ]
+    small[0].start()
+
+    def in_copy(n):
+        q, lo, hi = loads[n]
+        window, some = pl.ds(q * width, width), pl.ds(lo, hi - lo)
+        return [
+            pltpu.make_async_copy(
+                src.at[:, some, :, window], in_v.at[k, q, :, some], in_sem.at[n])
+            for k, src in enumerate((prec_hbm, flux_hbm))
+        ]
+
+    def in_wait(n):
+        q, lo, hi = loads[n]
+        here = in_v.at[:, q, :, pl.ds(lo, hi - lo)]
+        pltpu.make_async_copy(here, here, in_sem.at[n]).wait()
+
+    for n in range(len(loads)):
+        for copy in in_copy(n):
+            copy.start()
+
+    near = [(flip(e, bit), j) for bit in bits(ne)] + [(e, flip(j, bit)) for bit in bits(nb)]
+    barrier = pltpu.get_barrier_semaphore()
+    for other in near:
+        pl.semaphore_signal(barrier, inc=1, device_id=other, device_id_type=MESH)
+
+    def spread(k):
+        if k > 1:
+            pl.semaphore_wait(near_sem.at[k - 2], 1)
+        if k < len(near):
+            pl.semaphore_signal(
+                near_sem.at[k - 1], inc=1, device_id=near[k], device_id_type=MESH)
+
+    for copy in small[1:]:
+        copy.start()
     side = []
     for s in range(per_dest):
         for b in range(owned):
             row = s * owned + b
             window = pl.ds(s * block, block)
             side.append(pltpu.make_async_copy(
-                foot_hbm.at[b, :, window], foot_v.at[:, row, :], side_sem.at[0, row]))
+                foot_hbm.at[b, :, window], foot_v.at[:, row, :], side_sem.at[3]))
             side.append(pltpu.make_async_copy(
-                morph_hbm.at[b, :, window], morph_ref.at[:, row, :], side_sem.at[1, row]))
-
-    for q in range(chunks):
-        for copy in in_copy(q):
-            copy.start()
-
-    barrier = pltpu.get_barrier_semaphore()
-    total = ne * nb
-    mine = e * nb + j
-
-    def greet(d, carry):
-        other = lax.rem(mine + d, total)
-        pl.semaphore_signal(
-            barrier, inc=1, device_id=(other // nb, lax.rem(other, nb)), device_id_type=MESH
-        )
-        return carry
-
-    lax.fori_loop(1, total, greet, 0)
-
+                morph_hbm.at[b, :, window], morph_ref.at[:, row, :], side_sem.at[4]))
+
+    small[0].wait()
     square_r = lax.broadcasted_iota(jnp.int32, (every_blend, every_blend), 0)
     square_c = lax.broadcasted_iota(jnp.int32, (every_blend, every_blend), 1)
     lives = []
@@ -82,130 +118,122 @@
         column = jnp.sum(jnp.where(square_r == square_c, row, 0.0), axis=1, keepdims=True)
         lives.append(jnp.broadcast_to(column, (every_blend, LANES)))
 
-    def local_sum(q):
-        for copy in in_copy(q):
-            copy.wait()
+    def local_sum(i):
+        q, lo, hi = work[i]
+        for n, (r, start, _) in enumerate(loads):
+            if r == q and start == lo:
+                in_wait(n)
 
         def one(c, carry):
             for p in range(ne):
                 lanes = slice(p * LANES, (p + 1) * LANES)
-                py, px = p // nx, p % nx
+                py, px = p // 2, p % 2
                 num = None
                 for v in range(visits):
-                    w = prec_v[q, v, c, :, lanes].astype(f32) * lives[v]
-                    n = w * flux_v[q, v, c, :, lanes].astype(f32)
+                    w = in_v[0, q, v, c, :, lanes].astype(f32) * lives[v]
+                    n = w * in_v[1, q, v, c, :, lanes].astype(f32)
                     num, wsum = (n, w) if num is None else (num + n, wsum + w)
-                stage[0, q, px * ny + py, c] = num
-                stage[1, q, py * nx + px, c] = wsum
+                stage[0, q, px * 2 + py, c] = num
+                stage[1, q, py * 2 + px, c] = wsum
             return carry
 
-        lax.fori_loop(0, bands, one, 0)
-
-    def line(a, first):
-        along_x = (a == 0) == first
-        return (x, nx) if along_x else (y, ny)
-
-    def device_at(a, first, where):
-        along_x = (a == 0) == first
-        return (y * nx + where if along_x else where * nx + x, j)
-
-    def s1(a, q, d):
-        at, n = line(a, True)
-        other = line(a, False)[1]
-        to = lax.rem(at + d, n)
+        lax.fori_loop(lo, hi, one, 0)
+
+    along = (x, y)
+    across = (y, x)
+    mate = (near[0], near[1])
+
+    def s1(a, i):
+        q, lo, hi = work[i]
+        some = pl.ds(lo, hi - lo)
         return pltpu.make_async_remote_copy(
-            src_ref=stage.at[a, q, pl.ds(to * other, other)],
-            dst_ref=land1.at[a, q, d - 1],
-            send_sem=s1_send.at[a, q, d - 1], recv_sem=s1_recv.at[a, q, d - 1],
-            device_id=device_at(a, True, to), device_id_type=MESH,
+            src_ref=stage.at[a, q, pl.ds((1 - along[a]) * 2, 2), some],
+            dst_ref=land1.at[a, q, :, some],
+            send_sem=send_sem.at[0], recv_sem=s1_recv.at[i],
+            device_id=mate[a], device_id_type=MESH,
         )
 
-    def s2(a, q, d):
-        at, n = line(a, False)
-        to = lax.rem(at + d, n)
+    def s2(a, i):
+        q, lo, hi = work[i]
+        some = pl.ds(lo, hi - lo)
         return pltpu.make_async_remote_copy(
-            src_ref=part.at[a, q, to],
-            dst_ref=land2.at[a, q, d - 1],
-            send_sem=s2_send.at[a, q, d - 1], recv_sem=s2_recv.at[a, q, d - 1],
-            device_id=device_at(a, False, to), device_id_type=MESH,
+            src_ref=part.at[a, q, 1 - across[a], some],
+            dst_ref=land2.at[a, q, some],
+            send_sem=send_sem.at[1], recv_sem=s2_recv.at[i],
+            device_id=mate[1 - a], device_id_type=MESH,
         )
 
-    def s1_start(q):
+    def s1_start(i):
         for a in range(2):
-            for d in range(1, line(a, True)[1]):
-                s1(a, q, d).start()
-
-    def s2_start(q):
+            s1(a, i).start()
+
+    def s2_start(i):
+        q, lo, hi = work[i]
+        here = land1.at[:, q, :, pl.ds(lo, hi - lo)]
+        pltpu.make_async_copy(here, here, s1_recv.at[i]).wait()
+
+        def add(c, carry):
+            for a in range(2):
+                for o in range(2):
+                    part[a, q, o, c] = stage[a, q, along[a] * 2 + o, c] + land1[a, q, o, c]
+            return carry
+
+        lax.fori_loop(lo, hi, add, 0)
         for a in range(2):
-            at, n = line(a, True)
-            others = line(a, False)[1]
-            for d in range(1, n):
-                s1(a, q, d).wait_recv()
-
-            def add(c, carry):
-                for o in range(others):
-                    v = stage[a, q, at * others + o, c]
-                    for d in range(1, n):
-                        v = v + land1[a, q, d - 1, o, c]
-                    part[a, q, o, c] = v
-                return carry
-
-            lax.fori_loop(0, bands, add, 0)
-            for d in range(1, others):
-                s2(a, q, d).start()
+            s2(a, i).start()
 
     here = home_e == e
 
-    def landing(q):
+    def landing(i):
+        q, lo, hi = work[i]
         lanes = pl.ds(pl.multiple_of(e * LANES, LANES), LANES)
-        return pieces.at[q, :, :, home_slot, :, lanes]
-
-    def s3_local(q):
-        return pltpu.make_async_copy(final.at[q, j], landing(q), s3_recv.at[q])
-
-    def s3_remote(q, to):
+        return pieces.at[q, :, pl.ds(lo, hi - lo), home_slot, :, lanes]
+
+    def leaving(i, to):
+        q, lo, hi = work[i]
+        return final.at[q, to, :, pl.ds(lo, hi - lo)]
+
+    def s3_local(i):
+        return pltpu.make_async_copy(leaving(i, j), landing(i), s3_recv.at[work[i][0]])
+
+    def s3_remote(i, to):
         return pltpu.make_async_remote_copy(
-            src_ref=final.at[q, to], dst_ref=landing(q),
-            send_sem=s3_send.at[q, to], recv_sem=s3_recv.at[q],
+            src_ref=leaving(i, to), dst_ref=landing(i),
+            send_sem=send_sem.at[2], recv_sem=s3_recv.at[work[i][0]],
             device_id=(home_e, to), device_id_type=MESH,
         )
 
-    def s3_start(q):
-        for a in range(2):
-            at, n = line(a, False)
-            for d in range(1, n):
-                s2(a, q, d).wait_recv()
-
-            def add(c, carry):
-                v = part[a, q, at, c]
-                for d in range(1, n):
-                    v = v + land2[a, q, d - 1, c]
+    def s3_start(i):
+        q, lo, hi = work[i]
+        there = land2.at[:, q, pl.ds(lo, hi - lo)]
+        pltpu.make_async_copy(there, there, s2_recv.at[i]).wait()
+
+        def add(c, carry):
+            for a in range(2):
+                v = part[a, q, across[a], c] + land2[a, q, c]
                 for to in range(nb):
                     final[q, to, a, c] = v[to * owned : (to + 1) * owned, :]
-                return carry
-
-            lax.fori_loop(0, bands, add, 0)
+            return carry
+
+        lax.fori_loop(lo, hi, add, 0)
 
         def send(d, carry):
-            s3_remote(q, lax.rem(j + d, nb)).start()
+            s3_remote(i, lax.rem(j + d, nb)).start()
             return carry
 
         lax.fori_loop(1, nb, send, 0)
 
         @pl.when(here)
         def _():
-            s3_local(q).start()
+            s3_local(i).start()
 
         @pl.when(jnp.logical_not(here))
         def _():
-            s3_remote(q, j).start()
+            s3_remote(i, j).start()
 
     sub = lax.broadcasted_iota(jnp.int32, (held, LANES), 0)
     lane = lax.broadcasted_iota(jnp.int32, (held, LANES), 1)
-    count = jnp.zeros((held, LANES), jnp.int32)
-    for b in range(owned):
-        count = jnp.where(lax.rem(sub, owned) == b, count_ref[b], count)
-    live_count = count.astype(f32)
+    state = []
 
     def steps():
         for k in range(slots):
@@ -213,7 +241,7 @@
             for c in range(bands):
                 s = spectra[k, c]
                 norm = s * s if norm is None else norm + s * s
-            step_ref[k] = 1.0 / (1.0 + live_count * norm)
+            step_ref[k] = 1.0 / (1.0 + state[1] * norm)
 
     group = 2
 
@@ -223,7 +251,7 @@
         ]
 
         def masks(k):
-            live = jnp.where(count > k, 1.0, 0.0).astype(f32)
+            live = jnp.where(state[0] > k, 1.0, 0.0).astype(f32)
             return [foot_v[k, :, px].astype(f32) * live for px in runs]
 
         def residual(morph):
@@ -297,9 +325,22 @@
         to = lax.rem(e + d, ne)
         return pltpu.make_async_remote_copy(
             src_ref=sums.at[it, 0], dst_ref=sums.at[it, d],
-            send_sem=ps_send.at[it, d - 1], recv_sem=ps_recv.at[it, d - 1],
+            send_sem=send_sem.at[3], recv_sem=ps_recv.at[it],
             device_id=(to, j), device_id_type=MESH,
         )
+
+    def drain():
+        pltpu.make_async_copy(land1, land1, send_sem.at[0]).wait()
+        pltpu.make_async_copy(land2, land2, send_sem.at[1]).wait()
+
+        @pl.when(here)
+        def _():
+            some = final.at[:, pl.ds(0, nb - 1)]
+            pltpu.make_async_copy(some, some, send_sem.at[2]).wait()
+
+        @pl.when(jnp.logical_not(here))
+        def _():
+            pltpu.make_async_copy(final, final, send_sem.at[2]).wait()
 
     def update(it):
         packed = jnp.zeros((held, LANES), f32)
@@ -310,8 +351,10 @@
         sums[it, 0] = packed
         for d in range(1, ne):
             ps_copy(it, d).start()
-        for d in range(1, ne):
-            ps_copy(it, d).wait_recv()
+        if it == ITERS - 1:
+            drain()
+        arrived = sums.at[it, pl.ds(1, ne - 1)]
+        pltpu.make_async_copy(arrived, arrived, ps_recv.at[it]).wait()
         whole = None
         for o in range(ne):
             v = sums[it, lax.rem(e - o + ne, ne)]
@@ -323,20 +366,28 @@
         for k in range(slots):
             at = k * (bands + 1)
             norm = jnp.broadcast_to(whole[:, at + bands : at + bands + 1], (held, LANES))
-            scale = 1.0 / (1.0 + live_count * norm)
+            scale = 1.0 / (1.0 + state[1] * norm)
             for c in range(bands):
                 grad = jnp.broadcast_to(whole[:, at + c : at + c + 1], (held, LANES))
                 spectra[k, c] = jnp.maximum(0.0, spectra[k, c] + grad * scale)
 
     local_sum(0)
-    pl.semaphore_wait(barrier, total - 1)
+    pl.semaphore_wait(barrier, len(near))
     s1_start(0)
-    if chunks > 1:
-        local_sum(1)
-        s1_start(1)
+    spread(1)
+    for i in range(1, min(AHEAD, count_of)):
+        local_sum(i)
+        s1_start(i)
+        spread(i + 1)
     for copy in side:
         copy.start()
 
+    for copy in small[1:]:
+        copy.wait()
+    count = jnp.zeros((held, LANES), jnp.int32)
+    for b in range(owned):
+        count = jnp.where(lax.rem(sub, owned) == b, count_ref[b], count)
+    state.extend((count, count.astype(f32)))
     acc[...] = jnp.zeros_like(acc)
     for k in range(slots):
         for c in range(bands):
@@ -344,19 +395,22 @@
             spectra[k, c] = jnp.concatenate([start] * per_dest, axis=0)
     steps()
 
-    for q in range(chunks + 2):
-        if q < chunks:
-            s2_start(q)
-        if q + 2 < chunks:
-            local_sum(q + 2)
-            s1_start(q + 2)
-        if 0 <= q - 1 < chunks:
-            s3_start(q - 1)
-        if q == 2:
-            for copy in side:
-                copy.wait()
-        if 0 <= q - 2 < chunks:
-            finish(q - 2)
+    for k in range(min(AHEAD, count_of) + 1, len(near)):
+        spread(k)
+    for i in range(count_of + LAG):
+        if i < count_of:
+            s2_start(i)
+        if i + AHEAD < count_of:
+            local_sum(i + AHEAD)
+            s1_start(i + AHEAD)
+        if i == LAG:
+            spread(len(near))
+        if 0 <= i - LAG < count_of:
+            s3_start(i - LAG)
+    for done, copies in ((foot_v, 3), (morph_ref, 4)):
+        pltpu.make_async_copy(done, done, side_sem.at[copies]).wait()
+    for q in range(chunks):
+        finish(q)
 
     update(0)
     for it in range(1, ITERS):
@@ -375,42 +429,23 @@
             out = jnp.where(lane == k, spectra[k, c], out)
         spec_out[c] = out[0:owned, :slots]
 
-    for q in range(chunks):
-        for a in range(2):
-            for d in range(1, line(a, True)[1]):
-                s1(a, q, d).wait_send()
-            for d in range(1, line(a, False)[1]):
-                s2(a, q, d).wait_send()
-
-        def sent(d, carry, q=q):
-            s3_remote(q, lax.rem(j + d, nb)).wait_send()
-            return carry
-
-        lax.fori_loop(1, nb, sent, 0)
-
-        @pl.when(jnp.logical_not(here))
-        def _(q=q):
-            s3_remote(q, j).wait_send()
-
-    for it in range(ITERS):
-        for d in range(1, ne):
-            ps_copy(it, d).wait_send()
-
-
-def hand_over(coadd_in, spec_in, morph_in, coadd_out, spec_out, morph_out, sems, row_sems):
+    gone = sums.at[:, pl.ds(1, ne - 1)]
+    pltpu.make_async_copy(gone, gone, send_sem.at[3]).wait()
+
+
+def hand_over(coadd_in, spec_in, morph_in, coadd_out, spec_out, morph_out, sems):
     owned, _, pix_part = morph_out.shape
     _, held, block = morph_in.shape
-    copies = [
-        pltpu.make_async_copy(morph_in.at[:, row, :],
-                              morph_out.at[row % owned, :, pl.ds(row // owned * block, block)],
-                              row_sems.at[row])
-        for row in range(held)
-    ]
-    copies.append(pltpu.make_async_copy(coadd_in, coadd_out, sems.at[0]))
-    copies.append(pltpu.make_async_copy(spec_in, spec_out, sems.at[1]))
-    for copy in copies:
+    for row in range(held):
+        pltpu.make_async_copy(
+            morph_in.at[:, row, :],
+            morph_out.at[row % owned, :, pl.ds(row // owned * block, block)], sems.at[2]).start()
+    others = [pltpu.make_async_copy(coadd_in, coadd_out, sems.at[0]),
+              pltpu.make_async_copy(spec_in, spec_out, sems.at[1])]
+    for copy in others:
         copy.start()
-    for copy in copies:
+    pltpu.make_async_copy(morph_in, morph_in, sems.at[2]).wait()
+    for copy in others:
         copy.wait()
 
 
@@ -418,51 +453,50 @@
           morphology_init):
     visits, every_blend, bands, block = visit_flux.shape
     owned, slots, pix_part = morphology_init.shape
-    ny, nx = factors(ne)
     width = ne * LANES
     chunks = block // width
     per_dest = pix_part // block
     held = per_dest * owned
-    hop = max(nx, ny) - 1
-    line = max(nx, ny)
+    count_of = len(cut(chunks, bands))
+    loads = count_of // chunks + chunks - 1
     f32 = jnp.float32
-    vmem, smem, hbm = (pl.BlockSpec(memory_space=s) for s in (pltpu.VMEM, pltpu.SMEM, pl.ANY))
+    vmem, hbm = (pl.BlockSpec(memory_space=s) for s in (pltpu.VMEM, pl.ANY))
     dma = pltpu.SemaphoreType.DMA
     parts = pl.pallas_call(
-        functools.partial(coadd_kernel, ne=ne, nb=nb, ny=ny, nx=nx),
+        functools.partial(coadd_kernel, ne=ne, nb=nb),
         out_shape=(
             pltpu.VMEM((bands, owned, pix_part), f32),
             pltpu.VMEM((bands, owned, slots), f32),
             pltpu.VMEM((slots, held, block), f32),
         ),
-        in_specs=[hbm, hbm, vmem, hbm, smem, vmem, hbm],
+        in_specs=[hbm] * 7,
         out_specs=(vmem, vmem, vmem),
         scratch_shapes=[
-            pltpu.VMEM((chunks, visits, bands, every_blend, width), visit_flux.dtype),
-            pltpu.VMEM((chunks, visits, bands, every_blend, width), visit_precision.dtype),
+            pltpu.VMEM((2, chunks, visits, bands, every_blend, width), visit_flux.dtype),
+            pltpu.VMEM(visit_live.shape, jnp.int32),
             pltpu.VMEM((slots, held, block), jnp.int32),
+            pltpu.SMEM(source_count.shape, jnp.int32),
+            pltpu.VMEM((bands, owned, slots), f32),
             pltpu.VMEM((bands, held, block), f32),
             pltpu.VMEM((bands, held, block), f32),
             pltpu.VMEM((2, chunks, ne, bands, every_blend, LANES), f32),
-            pltpu.VMEM((2, chunks, hop, line, bands, every_blend, LANES), f32),
-            pltpu.VMEM((2, chunks, line, bands, every_blend, LANES), f32),
-            pltpu.VMEM((2, chunks, hop, bands, every_blend, LANES), f32),
+            pltpu.VMEM((2, chunks, 2, bands, every_blend, LANES), f32),
+            pltpu.VMEM((2, chunks, 2, bands, every_blend, LANES), f32),
+            pltpu.VMEM((2, chunks, bands, every_blend, LANES), f32),
             pltpu.VMEM((chunks, nb, 2, bands, owned, LANES), f32),
             pltpu.VMEM((chunks, 2, bands, per_dest, owned, width), f32),
             pltpu.VMEM((slots, bands, held, LANES), f32),
             pltpu.VMEM((slots, held, LANES), f32),
             pltpu.VMEM((slots, bands + 1, held, LANES), f32),
             pltpu.VMEM((ITERS, ne, held, LANES), f32),
-            dma((2, chunks)),
-            dma((2, held)),
-            dma((2, chunks, hop)),
-            dma((2, chunks, hop)),
-            dma((2, chunks, hop)),
-            dma((2, chunks, hop)),
-            dma((chunks, nb)),
+            dma((loads,)),
+            dma((5,)),
+            pltpu.SemaphoreType.REGULAR((len(bits(ne)) + len(bits(nb)) - 1,)),
+            dma((4,)),
+            dma((count_of,)),
+            dma((count_of,)),
             dma((chunks,)),
-            dma((ITERS, ne - 1)),
-            dma((ITERS, ne - 1)),
+            dma((ITERS,)),
         ],
         compiler_params=pltpu.CompilerParams(
             collective_id=0, has_side_effects=True, vmem_limit_bytes=58 * 2**20
@@ -478,7 +512,7 @@
         ),
         in_specs=[vmem] * 3,
         out_specs=(hbm,) * 3,
-        scratch_shapes=[dma((2,)), dma((held,))],
+        scratch_shapes=[dma((3,))],
         compiler_params=pltpu.CompilerParams(vmem_limit_bytes=8 * 2**20),
     )(*parts)
     return coadd.transpose(1, 0, 2), spectra.transpose(1, 2, 0), morphology
@@ -549,11 +583,12 @@
              morphology_init):
         block, bands = visit_flux.shape[3], visit_flux.shape[2]
         owned, pix_part = morphology_init.shape[0], morphology_init.shape[2]
-        ny, nx = factors(ne)
         fits = (
             block % (ne * LANES) == 0
             and pix_part % block == 0
-            and min(ny, nx) > 1
+            and factors(ne) == (2, 2)
+            and nb & (nb - 1) == 0
+            and AHEAD <= block // (ne * LANES) * bands
             and morphology_init.shape[1] * (bands + 1) <= LANES
         )
         run = functools.partial(fused, ne, nb) if fits else on_device

time: 57.6 us -> 53.6 us (0.931)
  Pallas kernels: 56.7 us -> 52.8 us
    pallas_call x1, Pallas kernels: 55.7 us -> 51.9 us  [fused(): pl.pallas_call(functools.partial(coadd_kernel, ne=ne, nb=nb), out_shape=(...]
where the time goes in v1:
time: 53.6 us; the launch traced here: 53.4 us
  Pallas kernels  52.8 us (99%)
  between operations  0.64 us (1%)
    pallas_call x1, Pallas kernels, fused(): pl.pallas_call(functools.partial(coadd_kernel, ne=ne, nb=nb), out_shape=(...  51.9 us

profile of v1, /device:TPU:0, one launch (start us, length us, event | category | flops | bytes accessed | tf_op | source)
XLA Modules:
  0.0 53.4 jit_solution(263922931122757829)
XLA Ops:
  0.6 51.9 %shard_map.94 = (f32[6,4,4096]{2,1,0:T(4,128)S(1)}, f32[6,4,8]{2,1,0:T(4,128)S(1)}, f32[8,8,2048]{2,1,0:T(8,128)S(1)}) custom-call(bf16[4,6,32,2048]{3,2,1,0:T(8,128)(2,1)} %bitcast.5, bf16[4,6,32,2048]{3,2,1,0:T(8,128)(2,1)} %bitcast.6, s32[4,32]{1,0:T(4,128)} %live_hbm.1, s32[4,8,4096]{2,1,0:T(8,128)} %foot_hbm.1, s32[4]{0:T(128)} %count_hbm.1, ...), custom_call_target="tpu_custom_call" | custom-call | tf_op jit(solution)/shard_map/pallas_call | solution.py:465
  52.5 0.9 %shard_map.95 = (f32[6,4,4096]{2,1,0:T(4,128)}, f32[6,4,8]{2,1,0:T(4,128)}, f32[4,8,4096]{2,1,0:T(8,128)}) custom-call(f32[6,4,4096]{2,1,0:T(4,128)S(1)} %get-tuple-element.9.coadd_in, f32[6,4,8]{2,1,0:T(4,128)S(1)} %get-tuple-element.10.spec_in, f32[8,8,2048]{2,1,0:T(8,128)S(1)} %get-tuple-element.11.morph_in), custom_call_target="tpu_custom_call" | custom-call | tf_op jit(solution)/shard_map/pallas_call | solution.py:506

commit v2 on v1

--- a/solution.py
+++ b/solution.py
@@ -12,8 +12,15 @@
 
 LANES = 128
 MESH = pl.DeviceIdType.MESH
-AHEAD = 3
-LAG = 2
+CUTS = 3
+AHEAD = 4
+LAG = 3
+ROUTES = (
+    (0, 0, 1, 6), (0, 2, 1, 2),
+    (1, 0, 0, 3), (1, 1, 0, 5),
+    (2, 0, 0, 4), (2, 2, 1, 2), (2, 3, 1, 2),
+    (3, 1, 0, 4), (3, 2, 1, 4),
+)
 
 
 def factors(count):
@@ -22,10 +29,31 @@
 
 
 def cut(chunks, bands):
-    half = max(1, bands // 2)
+    step = max(1, bands // CUTS)
     return [
-        (q, lo, min(bands, lo + half)) for q in range(chunks) for lo in range(0, bands, half)
+        (q, lo, min(bands, lo + step)) for q in range(chunks) for lo in range(0, bands, step)
     ]
+
+
+def plan():
+    unit, runs = {}, []
+    for t, p, first, n in ROUTES:
+        runs.append((first, p >> first & 1, p >> 1 - first & 1, t, p, unit.get(t, 0), n))
+        unit[t] = unit.get(t, 0) + n
+    slot, placed = 0, []
+    for first, one, two, t, p, u, n in sorted(runs):
+        placed.append((first, one, two, t, p, u, n, slot))
+        slot += n
+    return placed, slot
+
+
+def span(runs):
+    runs = list(runs)
+    return (min(r[7] for r in runs), sum(r[6] for r in runs)) if runs else (0, 0)
+
+
+def slots_of(runs):
+    return [r[7] + k for r in runs for k in range(r[6])]
 
 
 def bits(count):
@@ -40,7 +68,7 @@
     flux_hbm, prec_hbm, live_hbm, foot_hbm, count_hbm, spec_hbm, morph_hbm,
     coadd_ref, spec_out, morph_ref,
     in_v, live_ref, foot_v, count_ref, spec_ref, flux_c, cover,
-    stage, land1, part, land2, final, pieces, spectra, step_ref, acc, sums,
+    stage, land1, land2, final, pieces, spectra, step_ref, acc, sums,
     in_sem, side_sem, near_sem, send_sem, s1_recv, s2_recv, s3_recv, ps_recv,
     *, ne, nb,
 ):
@@ -57,6 +85,19 @@
     home_slot = j % per_dest
     f32 = jnp.float32
     work = cut(chunks, bands)
+    runs, slot_count = plan()
+    place = (x + home_e) % 2 + (y + home_e // 2) % 2 * 2
+    slot_at = []
+    for to in range(ne):
+        b0, b1 = (home_e + to) % 2, (home_e // 2 + to // 2) % 2
+        spots = []
+        for u in range(2 * ne):
+            t0, t1, t2, t3 = (
+                next(r[7] + u - r[5] for r in runs if r[3] == t and r[5] <= u < r[5] + r[6])
+                for t in range(ne)
+            )
+            spots.append(t0 + b0 * (t1 - t0) + b1 * (t2 - t0) + b0 * b1 * (t3 - t2 - t1 + t0))
+        slot_at.append(spots)
     count_of = len(work)
     loads = [w for w in work if w[0] == 0] + [(q, 0, bands) for q in range(1, chunks)]
 
@@ -125,111 +166,115 @@
                 in_wait(n)
 
         def one(c, carry):
-            for p in range(ne):
-                lanes = slice(p * LANES, (p + 1) * LANES)
-                py, px = p // 2, p % 2
+            for g in range(ne):
+                lanes = slice(g * LANES, (g + 1) * LANES)
                 num = None
                 for v in range(visits):
                     w = in_v[0, q, v, c, :, lanes].astype(f32) * lives[v]
                     n = w * in_v[1, q, v, c, :, lanes].astype(f32)
                     num, wsum = (n, w) if num is None else (num + n, wsum + w)
-                stage[0, q, px * 2 + py, c] = num
-                stage[1, q, py * 2 + px, c] = wsum
+                for k, total in enumerate((num, wsum)):
+                    for to in range(ne):
+                        stage[q, slot_at[to][k * ne + g], c] = total[to * held : (to + 1) * held, :]
             return carry
 
         lax.fori_loop(lo, hi, one, 0)
 
-    along = (x, y)
-    across = (y, x)
-    mate = (near[0], near[1])
-
-    def s1(a, i):
+    def at_place(act):
+        for p in range(ne):
+            @pl.when(place == p)
+            def _(p=p):
+                act(p)
+
+    def kept(p, first):
+        return [r for r in runs if r[0] == first and r[1] == p >> first & 1]
+
+    def given(p, first):
+        return [r for r in runs if r[0] == first and r[1] != p >> first & 1]
+
+    def passed(p, first):
+        return [r for r in kept(p, first) if r[2] != p >> 1 - first & 1]
+
+    def owned_at(p):
+        return [r for r in runs if r[4] == p]
+
+    def exchange(src, dst, i, sent, to, send, recv):
+        q, lo, hi = work[i]
+        first, n = span(sent)
+        if n:
+            piece = (q, pl.ds(first, n), pl.ds(lo, hi - lo))
+            pltpu.make_async_remote_copy(
+                src_ref=src.at[piece], dst_ref=dst.at[piece],
+                send_sem=send_sem.at[send], recv_sem=recv.at[i],
+                device_id=to, device_id_type=MESH,
+            ).start()
+
+    def arrive(ref, i, n, recv):
+        q, lo, hi = work[i]
+        if n:
+            here = ref.at[q, pl.ds(0, n), pl.ds(lo, hi - lo)]
+            pltpu.make_async_copy(here, here, recv.at[i]).wait()
+
+    def s1_start(i):
+        def act(p):
+            for first in range(2):
+                exchange(stage, land1, i, given(p, first), near[first], 0, s1_recv)
+
+        at_place(act)
+
+    def s2_start(i):
+        q, lo, hi = work[i]
+
+        def act(p):
+            mine = slots_of(kept(p, 0) + kept(p, 1))
+            arrive(land1, i, len(mine), s1_recv)
+
+            def add(c, carry):
+                for k in mine:
+                    stage[q, k, c] = stage[q, k, c] + land1[q, k, c]
+                return carry
+
+            lax.fori_loop(lo, hi, add, 0)
+            for first in range(2):
+                exchange(stage, land2, i, passed(p, first), near[1 - first], 1, s2_recv)
+
+        at_place(act)
+
+    def s3_start(i):
         q, lo, hi = work[i]
         some = pl.ds(lo, hi - lo)
-        return pltpu.make_async_remote_copy(
-            src_ref=stage.at[a, q, pl.ds((1 - along[a]) * 2, 2), some],
-            dst_ref=land1.at[a, q, :, some],
-            send_sem=send_sem.at[0], recv_sem=s1_recv.at[i],
-            device_id=mate[a], device_id_type=MESH,
-        )
-
-    def s2(a, i):
-        q, lo, hi = work[i]
-        some = pl.ds(lo, hi - lo)
-        return pltpu.make_async_remote_copy(
-            src_ref=part.at[a, q, 1 - across[a], some],
-            dst_ref=land2.at[a, q, some],
-            send_sem=send_sem.at[1], recv_sem=s2_recv.at[i],
-            device_id=mate[1 - a], device_id_type=MESH,
-        )
-
-    def s1_start(i):
-        for a in range(2):
-            s1(a, i).start()
-
-    def s2_start(i):
-        q, lo, hi = work[i]
-        here = land1.at[:, q, :, pl.ds(lo, hi - lo)]
-        pltpu.make_async_copy(here, here, s1_recv.at[i]).wait()
-
-        def add(c, carry):
-            for a in range(2):
-                for o in range(2):
-                    part[a, q, o, c] = stage[a, q, along[a] * 2 + o, c] + land1[a, q, o, c]
-            return carry
-
-        lax.fori_loop(lo, hi, add, 0)
-        for a in range(2):
-            s2(a, i).start()
-
-    here = home_e == e
-
-    def landing(i):
-        q, lo, hi = work[i]
-        lanes = pl.ds(pl.multiple_of(e * LANES, LANES), LANES)
-        return pieces.at[q, :, pl.ds(lo, hi - lo), home_slot, :, lanes]
-
-    def leaving(i, to):
-        q, lo, hi = work[i]
-        return final.at[q, to, :, pl.ds(lo, hi - lo)]
-
-    def s3_local(i):
-        return pltpu.make_async_copy(leaving(i, j), landing(i), s3_recv.at[work[i][0]])
-
-    def s3_remote(i, to):
-        return pltpu.make_async_remote_copy(
-            src_ref=leaving(i, to), dst_ref=landing(i),
-            send_sem=send_sem.at[2], recv_sem=s3_recv.at[work[i][0]],
-            device_id=(home_e, to), device_id_type=MESH,
-        )
-
-    def s3_start(i):
-        q, lo, hi = work[i]
-        there = land2.at[:, q, pl.ds(lo, hi - lo)]
-        pltpu.make_async_copy(there, there, s2_recv.at[i]).wait()
-
-        def add(c, carry):
-            for a in range(2):
-                v = part[a, q, across[a], c] + land2[a, q, c]
-                for to in range(nb):
-                    final[q, to, a, c] = v[to * owned : (to + 1) * owned, :]
-            return carry
-
-        lax.fori_loop(lo, hi, add, 0)
-
-        def send(d, carry):
-            s3_remote(i, lax.rem(j + d, nb)).start()
-            return carry
-
-        lax.fori_loop(1, nb, send, 0)
-
-        @pl.when(here)
-        def _():
-            s3_local(i).start()
-
-        @pl.when(jnp.logical_not(here))
-        def _():
-            s3_remote(i, j).start()
+
+        def act(p):
+            mine = slots_of(owned_at(p))
+            arrive(land2, i, len(mine), s2_recv)
+
+            def add(c, carry):
+                for k in mine:
+                    v = stage[q, k, c] + land2[q, k, c]
+                    for to in range(per_dest):
+                        final[q, to, k, c] = v[to * owned : (to + 1) * owned, :]
+                return carry
+
+            lax.fori_loop(lo, hi, add, 0)
+            for _, _, _, t, _, u, n, first in owned_at(p):
+                over = j
+                for bit in bits(ne):
+                    if t & bit:
+                        over = flip(over, bit * per_dest)
+                for d in (1, 0):
+                    to = flip(over, 1) if d else over
+                    src = final.at[q, to % per_dest, pl.ds(first, n), some]
+                    dst = pieces.at[q, home_slot, pl.ds(u, n), some]
+                    if p == 0 and t == 0 and d == 0:
+                        pltpu.make_async_copy(src, dst, s3_recv.at[q]).start()
+                    else:
+                        pltpu.make_async_remote_copy(
+                            src_ref=src, dst_ref=dst,
+                            send_sem=send_sem.at[2], recv_sem=s3_recv.at[q],
+                            device_id=(home_e, to), device_id_type=MESH,
+                        ).start()
+
+        at_place(act)
 
     sub = lax.broadcasted_iota(jnp.int32, (held, LANES), 0)
     lane = lax.broadcasted_iota(jnp.int32, (held, LANES), 1)
@@ -300,17 +345,18 @@
 
     def finish(q):
         pltpu.make_async_copy(pieces.at[q], pieces.at[q], s3_recv.at[q]).wait()
-        at = slice(q * width, (q + 1) * width)
 
         def unpack(c, carry):
             for s in range(per_dest):
                 rows = slice(s * owned, (s + 1) * owned)
-                wsum = pieces[q, 1, c, s]
-                inv = 1.0 / (1.0 + wsum)
-                flux = pieces[q, 0, c, s] * inv
-                coadd_ref[c, :, s * block + q * width : s * block + (q + 1) * width] = flux
-                flux_c[c, rows, at] = flux
-                cover[c, rows, at] = wsum * inv
+                for g in range(ne):
+                    wsum = pieces[q, s, ne + g, c]
+                    inv = 1.0 / (1.0 + wsum)
+                    flux = pieces[q, s, g, c] * inv
+                    px = q * width + g * LANES
+                    coadd_ref[c, :, s * block + px : s * block + px + LANES] = flux
+                    flux_c[c, rows, px : px + LANES] = flux
+                    cover[c, rows, px : px + LANES] = wsum * inv
             return carry
 
         lax.fori_loop(0, bands, unpack, 0)
@@ -330,17 +376,19 @@
         )
 
     def drain():
-        pltpu.make_async_copy(land1, land1, send_sem.at[0]).wait()
-        pltpu.make_async_copy(land2, land2, send_sem.at[1]).wait()
-
-        @pl.when(here)
-        def _():
-            some = final.at[:, pl.ds(0, nb - 1)]
-            pltpu.make_async_copy(some, some, send_sem.at[2]).wait()
-
-        @pl.when(jnp.logical_not(here))
-        def _():
-            pltpu.make_async_copy(final, final, send_sem.at[2]).wait()
+        def act(p):
+            for k, n in enumerate((
+                span(given(p, 0))[1] + span(given(p, 1))[1],
+                span(passed(p, 0))[1] + span(passed(p, 1))[1],
+            )):
+                if n:
+                    sent = stage.at[:, pl.ds(0, n)]
+                    pltpu.make_async_copy(sent, sent, send_sem.at[k]).wait()
+            n = sum(r[6] * (per_dest - (p == 0 and r[3] == 0)) for r in owned_at(p))
+            sent = final.at[:, 0, pl.ds(0, n)]
+            pltpu.make_async_copy(sent, sent, send_sem.at[2]).wait()
+
+        at_place(act)
 
     def update(it):
         packed = jnp.zeros((held, LANES), f32)
@@ -378,7 +426,8 @@
     for i in range(1, min(AHEAD, count_of)):
         local_sum(i)
         s1_start(i)
-        spread(i + 1)
+        if i + 1 < len(near):
+            spread(i + 1)
     for copy in side:
         copy.start()
 
@@ -459,6 +508,7 @@
     held = per_dest * owned
     count_of = len(cut(chunks, bands))
     loads = count_of // chunks + chunks - 1
+    slot_count = plan()[1]
     f32 = jnp.float32
     vmem, hbm = (pl.BlockSpec(memory_space=s) for s in (pltpu.VMEM, pl.ANY))
     dma = pltpu.SemaphoreType.DMA
@@ -479,12 +529,11 @@
             pltpu.VMEM((bands, owned, slots), f32),
             pltpu.VMEM((bands, held, block), f32),
             pltpu.VMEM((bands, held, block), f32),
-            pltpu.VMEM((2, chunks, ne, bands, every_blend, LANES), f32),
-            pltpu.VMEM((2, chunks, 2, bands, every_blend, LANES), f32),
-            pltpu.VMEM((2, chunks, 2, bands, every_blend, LANES), f32),
-            pltpu.VMEM((2, chunks, bands, every_blend, LANES), f32),
-            pltpu.VMEM((chunks, nb, 2, bands, owned, LANES), f32),
-            pltpu.VMEM((chunks, 2, bands, per_dest, owned, width), f32),
+            pltpu.VMEM((chunks, slot_count, bands, held, LANES), f32),
+            pltpu.VMEM((chunks, slot_count, bands, held, LANES), f32),
+            pltpu.VMEM((chunks, slot_count, bands, held, LANES), f32),
+            pltpu.VMEM((chunks, per_dest, slot_count, bands, owned, LANES), f32),
+            pltpu.VMEM((chunks, per_dest, 2 * ne, bands, owned, LANES), f32),
             pltpu.VMEM((slots, bands, held, LANES), f32),
             pltpu.VMEM((slots, held, LANES), f32),
             pltpu.VMEM((slots, bands + 1, held, LANES), f32),
@@ -587,7 +636,9 @@
             block % (ne * LANES) == 0
             and pix_part % block == 0
             and factors(ne) == (2, 2)
-            and nb & (nb - 1) == 0
+            and nb == 2 * ne
+            and pix_part == 2 * block
+            and visit_flux.shape[1] == owned * nb
             and AHEAD <= block // (ne * LANES) * bands
             and morphology_init.shape[1] * (bands + 1) <= LANES
         )

time: 53.6 us -> 52.3 us (0.976)
  Pallas kernels: 52.8 us -> 51.5 us
    pallas_call x1, Pallas kernels: 51.9 us -> 50.5 us  [fused(): pl.pallas_call(functools.partial(coadd_kernel, ne=ne, nb=nb), out_shape=(...]
where the time goes in v2:
time: 52.3 us; the launch traced here: 52.1 us
  Pallas kernels  51.5 us (98%)
  between operations  0.64 us (1%)
    pallas_call x1, Pallas kernels, fused(): pl.pallas_call(functools.partial(coadd_kernel, ne=ne, nb=nb), out_shape=(...  50.5 us

profile of v2, /device:TPU:0, one launch (start us, length us, event | category | flops | bytes accessed | tf_op | source)
XLA Modules:
  0.0 52.1 jit_solution(7639845952803986968)
XLA Ops:
  0.6 50.5 %shard_map.94 = (f32[6,4,4096]{2,1,0:T(4,128)S(1)}, f32[6,4,8]{2,1,0:T(4,128)S(1)}, f32[8,8,2048]{2,1,0:T(8,128)S(1)}) custom-call(bf16[4,6,32,2048]{3,2,1,0:T(8,128)(2,1)} %bitcast.5, bf16[4,6,32,2048]{3,2,1,0:T(8,128)(2,1)} %bitcast.6, s32[4,32]{1,0:T(4,128)} %live_hbm.1, s32[4,8,4096]{2,1,0:T(8,128)} %foot_hbm.1, s32[4]{0:T(128)} %count_hbm.1, ...), custom_call_target="tpu_custom_call" | custom-call | tf_op jit(solution)/shard_map/pallas_call | solution.py:515
  51.2 0.9 %shard_map.95 = (f32[6,4,4096]{2,1,0:T(4,128)}, f32[6,4,8]{2,1,0:T(4,128)}, f32[4,8,4096]{2,1,0:T(8,128)}) custom-call(f32[6,4,4096]{2,1,0:T(4,128)S(1)} %get-tuple-element.9.coadd_in, f32[6,4,8]{2,1,0:T(4,128)S(1)} %get-tuple-element.10.spec_in, f32[8,8,2048]{2,1,0:T(8,128)S(1)} %get-tuple-element.11.morph_in), custom_call_target="tpu_custom_call" | custom-call | tf_op jit(solution)/shard_map/pallas_call | solution.py:555

commit v3 on v2

--- a/solution.py
+++ b/solution.py
@@ -256,16 +256,19 @@
                 return carry
 
             lax.fori_loop(lo, hi, add, 0)
-            for _, _, _, t, _, u, n, first in owned_at(p):
-                over = j
-                for bit in bits(ne):
-                    if t & bit:
-                        over = flip(over, bit * per_dest)
-                for d in (1, 0):
-                    to = flip(over, 1) if d else over
-                    src = final.at[q, to % per_dest, pl.ds(first, n), some]
+            for order in range(per_dest):
+                for _, _, _, t, _, u, n, first in sorted(owned_at(p), key=lambda r: -r[3]):
+                    over = j
+                    for bit in bits(ne):
+                        if t & bit:
+                            over = flip(over, bit * per_dest)
+                    stays = p == 0 and t == 0
+                    to = flip(over, 1) if stays else over - home_slot + order
+                    core = to % per_dest if stays else order
+                    src = final.at[q, core, pl.ds(first, n), some]
                     dst = pieces.at[q, home_slot, pl.ds(u, n), some]
-                    if p == 0 and t == 0 and d == 0:
+                    if stays and order:
+                        src = final.at[q, home_slot, pl.ds(first, n), some]
                         pltpu.make_async_copy(src, dst, s3_recv.at[q]).start()
                     else:
                         pltpu.make_async_remote_copy(

time: 52.3 us -> 52 us (level)
  no operation moved by 1% of the time
where the time goes in v3:
time: 52 us; the launch traced here: 51.8 us
  Pallas kernels  51.2 us (98%)
  between operations  0.64 us (1%)
    pallas_call x1, Pallas kernels, fused(): pl.pallas_call(functools.partial(coadd_kernel, ne=ne, nb=nb), out_shape=(...  50.2 us

profile of v3, /device:TPU:0, one launch (start us, length us, event | category | flops | bytes accessed | tf_op | source)
XLA Modules:
  0.0 51.8 jit_solution(745113417054385989)
XLA Ops:
  0.6 50.2 %shard_map.94 = (f32[6,4,4096]{2,1,0:T(4,128)S(1)}, f32[6,4,8]{2,1,0:T(4,128)S(1)}, f32[8,8,2048]{2,1,0:T(8,128)S(1)}) custom-call(bf16[4,6,32,2048]{3,2,1,0:T(8,128)(2,1)} %bitcast.5, bf16[4,6,32,2048]{3,2,1,0:T(8,128)(2,1)} %bitcast.6, s32[4,32]{1,0:T(4,128)} %live_hbm.1, s32[4,8,4096]{2,1,0:T(8,128)} %foot_hbm.1, s32[4]{0:T(128)} %count_hbm.1, ...), custom_call_target="tpu_custom_call" | custom-call | tf_op jit(solution)/shard_map/pallas_call | solution.py:518
  50.9 0.9 %shard_map.95 = (f32[6,4,4096]{2,1,0:T(4,128)}, f32[6,4,8]{2,1,0:T(4,128)}, f32[4,8,4096]{2,1,0:T(8,128)}) custom-call(f32[6,4,4096]{2,1,0:T(4,128)S(1)} %get-tuple-element.9.coadd_in, f32[6,4,8]{2,1,0:T(4,128)S(1)} %get-tuple-element.10.spec_in, f32[8,8,2048]{2,1,0:T(8,128)S(1)} %get-tuple-element.11.morph_in), custom_call_target="tpu_custom_call" | custom-call | tf_op jit(solution)/shard_map/pallas_call | solution.py:558

commit v4 on v3

--- a/solution.py
+++ b/solution.py
@@ -15,12 +15,7 @@
 CUTS = 3
 AHEAD = 4
 LAG = 3
-ROUTES = (
-    (0, 0, 1, 6), (0, 2, 1, 2),
-    (1, 0, 0, 3), (1, 1, 0, 5),
-    (2, 0, 0, 4), (2, 2, 1, 2), (2, 3, 1, 2),
-    (3, 1, 0, 4), (3, 2, 1, 4),
-)
+ROUTES = ((0, 0, 0, 6), (0, 1, 0, 1), (0, 2, 1, 1), (1, 0, 1, 8), (2, 1, 0, 1), (2, 2, 1, 7), (3, 1, 0, 5), (3, 3, 0, 3))
 
 
 def factors(count):

time: 52 us -> 52 us (level)
  no operation moved by 1% of the time
where the time goes in v4:
time: 52 us; the launch traced here: 51.8 us
  Pallas kernels  51.2 us (98%)
  between operations  0.64 us (1%)
    pallas_call x1, Pallas kernels, fused(): pl.pallas_call(functools.partial(coadd_kernel, ne=ne, nb=nb), out_shape=(...  50.2 us

profile of v4, /device:TPU:0, one launch (start us, length us, event | category | flops | bytes accessed | tf_op | source)
XLA Modules:
  0.0 51.8 jit_solution(4387310417758800975)
XLA Ops:
  0.6 50.2 %shard_map.94 = (f32[6,4,4096]{2,1,0:T(4,128)S(1)}, f32[6,4,8]{2,1,0:T(4,128)S(1)}, f32[8,8,2048]{2,1,0:T(8,128)S(1)}) custom-call(bf16[4,6,32,2048]{3,2,1,0:T(8,128)(2,1)} %bitcast.5, bf16[4,6,32,2048]{3,2,1,0:T(8,128)(2,1)} %bitcast.6, s32[4,32]{1,0:T(4,128)} %live_hbm.1, s32[4,8,4096]{2,1,0:T(8,128)} %foot_hbm.1, s32[4]{0:T(128)} %count_hbm.1, ...), custom_call_target="tpu_custom_call" | custom-call | tf_op jit(solution)/shard_map/pallas_call | solution.py:513
  50.9 0.9 %shard_map.95 = (f32[6,4,4096]{2,1,0:T(4,128)}, f32[6,4,8]{2,1,0:T(4,128)}, f32[4,8,4096]{2,1,0:T(8,128)}) custom-call(f32[6,4,4096]{2,1,0:T(4,128)S(1)} %get-tuple-element.9.coadd_in, f32[6,4,8]{2,1,0:T(4,128)S(1)} %get-tuple-element.10.spec_in, f32[8,8,2048]{2,1,0:T(8,128)S(1)} %get-tuple-element.11.morph_in), custom_call_target="tpu_custom_call" | custom-call | tf_op jit(solution)/shard_map/pallas_call | solution.py:553
